TPU v7x, 8 devices: a whole 2x2x1 slice. The times are simulated.
8 devices in a mesh: dp: 2 (over z, y), cp: 4 (over x, core).
Axes of the slice: x: 2, y: 2, z: 1, core: 2. Of those that a mesh axis runs over, the one named last changes fastest.
Arguments:
- queries: bfloat16 [64, 512, 10, 256], P('dp', 'cp'), parts along dimension 0
- key_states: bfloat16 [64, 512, 256], P('dp', 'cp'), parts along dimension 0
- value_states: bfloat16 [64, 512, 256], P('dp', 'cp'), parts along dimension 0
- segment_ids: int32 [64, 512], P('dp', 'cp'), parts along dimension 0
Outputs:
- output 1: bfloat16 [64, 512, 10, 256], P('dp', 'cp'), parts along dimension 0
- output 2: float32 [64, 512, 10], P('dp', 'cp'), parts along dimension 0
There are 2 independent parts. A program takes and returns all parts, laid end to end along the dimension named above; each array names one.
All inputs are finite; a program needn't handle non-finite values.
Results may differ from a plain program's by a relative error of at most 0.00326493.
Values are sent between devices in bfloat16 or wider.
A program may use at most 1 GiB of HBM per device.

v0:
```python
import functools

import jax
import jax.numpy as jnp
from jax import lax
from jax.experimental import pallas as pl
from jax.experimental.pallas import tpu as pltpu
from jax.sharding import PartitionSpec as P


CHUNKS = (6, 10, 9, 5, 2)
BOUNDS = tuple(sum(CHUNKS[:n]) for n in range(len(CHUNKS) + 1))
GROUP = 2
DEPTH = 3
LOG2E = 1.4426950408889634

ACROSS = [(0, 2), (1, 3)]
BESIDE = [(0, 1), (2, 3)]
SWAP = [(2, 3), (3, 2)]


def pack_kernel(ranges, tails, seg_ref, k_ref, v_ref, *rest):
    count = len(ranges)
    outs, (k_scr, v_scr, z_scr, in_sem, out_sem) = rest[:count], rest[count:]
    piece = k_ref.shape[1]
    first = min(a for a, _ in ranges)
    last = max(b for _, b in ranges)
    loads = [
        pltpu.make_async_copy(src.at[pl.ds(first, last - first)], dst.at[pl.ds(first, last - first)], in_sem.at[i])
        for i, (src, dst) in enumerate(((k_ref, k_scr), (v_ref, v_scr)))
    ]
    for load in loads:
        load.start()
    here = jnp.sum((seg_ref[...] == 0).astype(jnp.float32), axis=1, keepdims=True)
    z_scr[...] = jnp.broadcast_to(here, z_scr.shape).astype(jnp.bfloat16)
    for load in loads:
        load.wait()
    for out, (a, b), tail in zip(outs, ranges, tails):
        @pl.loop(0, b - a)
        def _(i):
            for half, src in enumerate((k_scr, v_scr)):
                pltpu.make_async_copy(
                    src.at[a + i], out.at[pl.ds(pl.multiple_of((2 * i + half) * piece, piece), piece)], out_sem
                ).start()

        if tail:
            pltpu.make_async_copy(z_scr, out.at[pl.ds((b - a) * 2 * piece, z_scr.shape[0])], out_sem).start()
    for out in outs:
        pltpu.make_async_copy(out, out, out_sem).wait()


def pack(ranges, tails, seg, k, v):
    batch, piece, head = k.shape
    return pl.pallas_call(
        functools.partial(pack_kernel, ranges, tails),
        in_specs=[pl.BlockSpec(memory_space=pltpu.VMEM)] + [pl.BlockSpec(memory_space=pl.ANY)] * 2,
        out_specs=[pl.BlockSpec(memory_space=pl.ANY)] * len(ranges),
        out_shape=[
            jax.ShapeDtypeStruct(((b - a) * 2 * piece + (batch if tail else 0), head), jnp.bfloat16)
            for (a, b), tail in zip(ranges, tails)
        ],
        scratch_shapes=[
            pltpu.VMEM(k.shape, jnp.bfloat16),
            pltpu.VMEM(k.shape, jnp.bfloat16),
            pltpu.VMEM((batch, head), jnp.bfloat16),
            pltpu.SemaphoreType.DMA((2,)),
            pltpu.SemaphoreType.DMA,
        ],
        cost_estimate=pl.CostEstimate(flops=1 << 20, bytes_accessed=4 * k.size, transcendentals=0),
    )(seg, k, v)


def attend_kernel(first, base, size, s_hbm, q_ref, k_ref, v_ref, near_ref, fara_ref, farb_ref, *rest):
    if first:
        o_ref, lse_ref, *scratch = rest
    else:
        _, lse_in, o_ref, lse_ref, *scratch = rest
    s_ref, q_buf, k_buf, v_buf, o_buf, s_sem, kv_sem, q_sem, o_sem = scratch
    depth, heads, piece, head = q_buf.shape
    groups = heads // GROUP
    width = GROUP * piece
    scale = head ** -0.5
    me = lax.axis_index("cp")
    odd = lax.rem(me, 2)
    scalars = pltpu.make_async_copy(s_hbm, s_ref, s_sem)
    scalars.start()

    def kv_loads(step):
        slot = lax.rem(step, depth)
        seq = base + step
        there = pl.ds(pl.multiple_of(jnp.where(odd == 1, 1, 3) * piece, piece), piece)
        out = []
        for half, (ref, buf) in enumerate(((k_ref, k_buf), (v_ref, v_buf))):
            rows = pl.ds(pl.multiple_of((2 * seq + half) * piece, piece), piece)
            out.append(pltpu.make_async_copy(ref.at[seq], buf.at[slot, pl.ds(0, piece)], kv_sem.at[slot]))
            out.append(pltpu.make_async_copy(near_ref.at[rows], buf.at[slot, there], kv_sem.at[slot]))
        return out

    def part(g):
        return pl.ds(g * GROUP, GROUP)

    def q_load(step, g):
        slot = lax.rem(step, depth)
        return pltpu.make_async_copy(q_ref.at[base + step, part(g)], q_buf.at[slot, part(g)], q_sem.at[slot, g])

    def o_store(step, g):
        slot = lax.rem(step, 2)
        return pltpu.make_async_copy(o_buf.at[slot, part(g)], o_ref.at[base + step, part(g)], o_sem.at[slot, g])

    def load(step):
        for copy in kv_loads(step):
            copy.start()
        for g in range(groups):
            q_load(step, g).start()

    def place(step):
        slot = lax.rem(step, depth)
        for ref, block in ((fara_ref, 2), (farb_ref, jnp.where(odd == 1, 3, 1))):
            there = pl.ds(pl.multiple_of(block * piece, piece), piece)
            for half, buf in enumerate((k_buf, v_buf)):
                buf[slot, there] = ref[pl.ds(pl.multiple_of((2 * step + half) * piece, piece), piece)]

    def run(count, step, cut):
        seq = base + step
        slot, out = lax.rem(step, depth), lax.rem(step, 2)
        keys = count * piece
        lane = lax.broadcasted_iota(jnp.int32, (piece, piece), 1)
        row = lax.broadcasted_iota(jnp.int32, (piece, piece), 0)
        low = jnp.maximum(jnp.where(row >= cut, cut, -keys), -me * piece)
        caps = [
            jnp.where((lane - n * piece <= row) & (lane - n * piece >= low), jnp.inf, -jnp.inf) for n in range(count)
        ]
        cap = jnp.concatenate([jnp.concatenate(caps, axis=1)] * GROUP, axis=0)
        logs = jnp.zeros((piece, piece), jnp.float32)

        def scores(g):
            q = q_buf[slot, g * GROUP:(g + 1) * GROUP].reshape(width, head)
            s = lax.dot_general(q, k_buf[slot, :keys], (((1,), (1,)), ((), ())), preferred_element_type=jnp.float32)
            s = jnp.minimum(s, cap)
            return s, jnp.max(s, axis=1, keepdims=True)

        def weigh(s, m):
            p = jnp.exp2((s - m) * (scale * LOG2E))
            return p.astype(jnp.bfloat16), m, jnp.sum(p, axis=1, keepdims=True)

        def finish(g, logs, p, m, l):
            o = jnp.dot(p, v_buf[slot, :keys], preferred_element_type=jnp.float32) * (1.0 / l)
            o_buf[out, g * GROUP:(g + 1) * GROUP] = o.astype(jnp.bfloat16).reshape(GROUP, piece, head)
            e = m * scale + jnp.log(l)
            for j in range(GROUP):
                logs = jnp.where(lane == g * GROUP + j, e[j * piece:(j + 1) * piece], logs)
            return logs

        now, before = scores(0), None
        for g in range(groups):
            later = scores(g + 1) if g + 1 < groups else None
            if before is not None:
                logs = finish(g - 1, logs, *before)
            before, now = weigh(*now), later
        logs = finish(groups - 1, logs, *before)
        lse_ref[:, pl.ds(seq, 1), :] = logs.T[:heads][:, None, :]

    load(0)
    if size > 1:
        load(1)
    if not first:
        lse_ref[...] = lse_in[...]
    scalars.wait()

    @pl.loop(0, size)
    def _(step):
        for copy in kv_loads(step):
            copy.wait()
        for g in range(groups):
            q_load(step, g).wait()

        @pl.when(step + 2 < size)
        def _():
            load(step + 2)

        @pl.when(step >= 2)
        def _():
            for g in range(groups):
                o_store(step - 2, g).wait()

        place(step)
        run(4, step, s_ref[base + step])
        for g in range(groups):
            o_store(step, g).start()

    for step in range(max(size - 2, 0), size):
        for g in range(groups):
            o_store(step, g).wait()


def attend(n, scalars, q, k, v, near, fara, farb, prev):
    batch, heads, piece, head = q.shape
    base, size = BOUNDS[n], CHUNKS[n]
    first = prev is None
    hbm = pl.BlockSpec(memory_space=pltpu.HBM)
    vmem = pl.BlockSpec(memory_space=pltpu.VMEM)
    in_specs = [hbm] * 5 + [vmem] * 2
    scalars, q, k, v, near = (pltpu.with_memory_space_constraint(x, pltpu.HBM) for x in (scalars, q, k, v, near))
    args = [scalars, q, k, v, near, fara, farb]
    aliases = {}
    if not first:
        in_specs += [hbm, vmem]
        args += list(prev)
        aliases = {7: 0}
    return pl.pallas_call(
        functools.partial(attend_kernel, first, base, size),
        in_specs=in_specs,
        out_specs=[hbm, vmem],
        scratch_shapes=[
            pltpu.SMEM(scalars.shape, jnp.int32),
            pltpu.VMEM((DEPTH, heads, piece, head), jnp.bfloat16),
            pltpu.VMEM((DEPTH, 4 * piece, head), jnp.bfloat16),
            pltpu.VMEM((DEPTH, 4 * piece, head), jnp.bfloat16),
            pltpu.VMEM((2, heads, piece, head), jnp.bfloat16),
            pltpu.SemaphoreType.DMA,
            pltpu.SemaphoreType.DMA((DEPTH,)),
            pltpu.SemaphoreType.DMA((DEPTH, heads // GROUP)),
            pltpu.SemaphoreType.DMA((2, heads // GROUP)),
        ],
        out_shape=[
            jax.ShapeDtypeStruct(q.shape, jnp.bfloat16),
            jax.ShapeDtypeStruct((heads, batch, piece), jnp.float32),
        ],
        input_output_aliases=aliases,
        compiler_params=pltpu.CompilerParams(vmem_limit_bytes=32 << 20),
        cost_estimate=pl.CostEstimate(
            flops=size * heads * piece * 4 * piece * head * 4,
            bytes_accessed=size * heads * piece * head * 4,
            transcendentals=0,
        ),
    )(*args)


def shift(x, pairs):
    return lax.ppermute(x, "cp", pairs)


def solution(mesh):
    def local(q_loc, k_loc, v_loc, seg_loc):
        batch, piece, _, _ = q_loc.shape
        me = lax.axis_index("cp")
        q = jnp.transpose(q_loc, (0, 2, 1, 3))
        ranges = tuple(zip(BOUNDS[:-1], BOUNDS[1:]))
        sends = pack(ranges[:1], (True,), seg_loc, k_loc, v_loc)
        *more, whole = pack(ranges[1:] + ((0, batch),), (False,) * len(ranges[1:]) + (True,), seg_loc, k_loc, v_loc)
        sends = list(sends) + more
        fara = [shift(x, ACROSS) for x in sends]
        near = shift(whole, BESIDE)
        farb = [shift(x, SWAP) for x in fara]

        def zeros(packed, there):
            return jnp.where(there, packed[-batch:, 0].astype(jnp.int32), 0)

        odd, upper = me % 2 == 1, me >= 2
        cuts = zeros(whole, True) + zeros(near, odd) + zeros(fara[0], upper) + zeros(farb[0], upper)
        need = jnp.where(cuts <= me * piece, me - cuts // piece, me) + 1
        scalars = jnp.concatenate([cuts - me * piece, need.astype(jnp.int32)])
        state = None
        for n in range(len(CHUNKS)):
            state = attend(n, scalars, q, k_loc, v_loc, near, fara[n], farb[n], state)
        out, lse = state
        return jnp.transpose(out, (0, 2, 1, 3)), jnp.transpose(lse, (1, 2, 0))

    return jax.shard_map(
        local,
        mesh=mesh,
        in_specs=(P("dp", "cp", None, None), P("dp", "cp", None), P("dp", "cp", None), P("dp", "cp")),
        out_specs=(P("dp", "cp", None, None), P("dp", "cp", None)),
        check_vma=False,
    )
```

profile of v0, /device:TPU:7, one launch (start us, length us, event | category | flops | bytes accessed | tf_op | source)
XLA Modules:
  0.0 171.3 jit_solution(5283486024941715415)
XLA Ops:
  0.6 5.9 %shard_map.59 = (bf16[2560,256]{1,0:T(8,128)(2,1)}, bf16[2304,256]{1,0:T(8,128)(2,1)}, bf16[1280,256]{1,0:T(8,128)(2,1)}, bf16[512,256]{1,0:T(8,128)(2,1)}, bf16[8224,256]{1,0:T(8,128)(2,1)}) custom-call(s32[32,128]{1,0:T(8,128)} %seg_ref.3, bf16[32,128,256]{2,1,0:T(8,128)(2,1)} %k_ref.13, bf16[32,128,256]{2,1,0:T(8,128)(2,1)} %v_ref.13), custom_call_target="tpu_custom_call" | custom-call | flops 1048576 | bytes 4194304 | tf_op jit(solution)/shard_map/pallas_call | solution.py:54
  6.6 0.0 copy-start.2
  6.6 1.4 collective-permute-start
  8.0 1.3 collective-permute-start.9
  9.3 2.8 %shard_map.60 = bf16[1568,256]{1,0:T(8,128)(2,1)} custom-call(s32[32,128]{1,0:T(8,128)} %seg_ref.3, bf16[32,128,256]{2,1,0:T(8,128)(2,1)} %k_ref.13, bf16[32,128,256]{2,1,0:T(8,128)(2,1)} %v_ref.13), custom_call_target="tpu_custom_call" | custom-call | flops 1048576 | bytes 4194304 | tf_op jit(solution)/shard_map/pallas_call | solution.py:54
  12.1 1.3 collective-permute-start.1
  13.4 1.3 collective-permute-start.7
  14.7 0.0 copy-done.2
  14.8 1.3 collective-permute-start.3
  16.1 38.5 %collective-permute-done.1.fara_ref = bf16[1568,256]{1,0:T(8,128)(2,1)S(1)} collective-permute-done((bf16[1568,256]{1,0:T(8,128)(2,1)}, bf16[1568,256]{1,0:T(8,128)(2,1)S(1)}, u32[]{:S(2)}, u32[]{:S(2)}) %collective-permute-start.1) | collective-permute-done | bytes 802848 | tf_op jit(solution)/shard_map/ppermute | solution.py:240
  54.6 9.4 %collective-permute-start.2 = (bf16[1568,256]{1,0:T(8,128)(2,1)S(1)}, bf16[1568,256]{1,0:T(8,128)(2,1)}, u32[]{:S(2)}, u32[]{:S(2)}) collective-permute-start(bf16[1568,256]{1,0:T(8,128)(2,1)S(1)} %collective-permute-done.1.fara_ref), channel_id=1, source_target_pairs={{2,3},{3,2},{6,7},{7,6}} | collective-permute-start | bytes 2408456 | tf_op jit(solution)/shard_map/ppermute | solution.py:240
  63.9 21.6 %collective-permute-done.3.fara_ref = bf16[512,256]{1,0:T(8,128)(2,1)S(1)} collective-permute-done((bf16[512,256]{1,0:T(8,128)(2,1)S(1)}, bf16[512,256]{1,0:T(8,128)(2,1)S(1)}, u32[]{:S(2)}, u32[]{:S(2)}) %collective-permute-start.3) | collective-permute-done | bytes 262176 | tf_op jit(solution)/shard_map/ppermute | solution.py:240
  85.6 0.0 copy-start
  85.6 1.3 collective-permute-start.5
  86.9 0.0 copy-done
  86.9 0.0 collective-permute-done.9.fara_ref
  86.9 5.7 %collective-permute-start.10 = (bf16[2560,256]{1,0:T(8,128)(2,1)S(1)}, bf16[2560,256]{1,0:T(8,128)(2,1)S(1)}, u32[]{:S(2)}, u32[]{:S(2)}) collective-permute-start(bf16[2560,256]{1,0:T(8,128)(2,1)S(1)} %collective-permute-done.9.fara_ref), channel_id=1, source_target_pairs={{2,3},{3,2},{6,7},{7,6}} | collective-permute-start | bytes 3932168 | tf_op jit(solution)/shard_map/ppermute | solution.py:240
  92.7 7.6 %collective-permute-done.5.fara_ref = bf16[1280,256]{1,0:T(8,128)(2,1)} collective-permute-done((bf16[1280,256]{1,0:T(8,128)(2,1)}, bf16[1280,256]{1,0:T(8,128)(2,1)}, u32[]{:S(2)}, u32[]{:S(2)}) %collective-permute-start.5) | collective-permute-done | bytes 655392 | tf_op jit(solution)/shard_map/ppermute | solution.py:240
  100.3 6.6 %collective-permute-start.4 = (bf16[512,256]{1,0:T(8,128)(2,1)}, bf16[512,256]{1,0:T(8,128)(2,1)S(1)}, u32[]{:S(2)}, u32[]{:S(2)}) collective-permute-start(bf16[512,256]{1,0:T(8,128)(2,1)} %copy-done), channel_id=1, source_target_pairs={{2,3},{3,2},{6,7},{7,6}} | collective-permute-start | bytes 786440 | tf_op jit(solution)/shard_map/ppermute | solution.py:240
  106.8 0.0 collective-permute-done.7.fara_ref
  106.9 1.9 %collective-permute-start.6 = (bf16[1280,256]{1,0:T(8,128)(2,1)}, bf16[1280,256]{1,0:T(8,128)(2,1)S(1)}, u32[]{:S(2)}, u32[]{:S(2)}) collective-permute-start(bf16[1280,256]{1,0:T(8,128)(2,1)} %collective-permute-done.5.fara_ref), channel_id=1, source_target_pairs={{2,3},{3,2},{6,7},{7,6}} | collective-permute-start | bytes 1966088 | tf_op jit(solution)/shard_map/ppermute | solution.py:240
  108.8 0.0 collective-permute-done.2.farb_ref
  108.8 2.4 %collective-permute-start.8 = (bf16[2304,256]{1,0:T(8,128)(2,1)}, bf16[2304,256]{1,0:T(8,128)(2,1)S(1)}, u32[]{:S(2)}, u32[]{:S(2)}) collective-permute-start(bf16[2304,256]{1,0:T(8,128)(2,1)} %collective-permute-done.7.fara_ref), channel_id=1, source_target_pairs={{2,3},{3,2},{6,7},{7,6}} | collective-permute-start | bytes 3538952 | tf_op jit(solution)/shard_map/ppermute | solution.py:240
  111.2 0.0 collective-permute-done.near_ref
  111.2 0.9 add_reduce_fusion
  112.1 0.6 pad_add_fusion.s_hbm
  112.7 11.5 %shard_map.61 = (bf16[32,10,128,256]{3,2,1,0:T(8,128)(2,1)}, f32[10,32,128]{2,1,0:T(8,128)S(1)}) custom-call(s32[64]{0:T(128)} %pad_add_fusion.s_hbm, bf16[32,10,128,256]{3,2,1,0:T(8,128)(2,1)} %bitcast.3, bf16[32,128,256]{2,1,0:T(8,128)(2,1)} %k_ref.13, bf16[32,128,256]{2,1,0:T(8,128)(2,1)} %v_ref.13, bf16[8224,256]{1,0:T(8,128)(2,1)} %collective-permute-done.near_ref, ...), custom_call_target="tpu_custom_call" | custom-call | flops 4026531840 | bytes 7864320 | tf_op jit(solution)/shard_map/pallas_call | solution.py:210
  124.1 0.0 collective-permute-done.10.farb_ref
  124.1 15.7 %shard_map.62 = (bf16[32,10,128,256]{3,2,1,0:T(8,128)(2,1)}, f32[10,32,128]{2,1,0:T(8,128)S(1)}) custom-call(s32[64]{0:T(128)} %pad_add_fusion.s_hbm, bf16[32,10,128,256]{3,2,1,0:T(8,128)(2,1)} %bitcast.4, bf16[32,128,256]{2,1,0:T(8,128)(2,1)} %k_ref.13, bf16[32,128,256]{2,1,0:T(8,128)(2,1)} %v_ref.13, ...), custom_call_target="tpu_custom_call", output_to_operand_aliasing={{0}: (7, {})} | custom-call | flops 6710886400 | bytes 13107200 | tf_op jit(solution)/shard_map/pallas_call | solution.py:210
  139.9 0.0 collective-permute-done.8.farb_ref
  139.9 15.6 %shard_map.63 = (bf16[32,10,128,256]{3,2,1,0:T(8,128)(2,1)}, f32[10,32,128]{2,1,0:T(8,128)S(1)}) custom-call(s32[64]{0:T(128)} %pad_add_fusion.s_hbm, bf16[32,10,128,256]{3,2,1,0:T(8,128)(2,1)} %bitcast.5, bf16[32,128,256]{2,1,0:T(8,128)(2,1)} %k_ref.13, bf16[32,128,256]{2,1,0:T(8,128)(2,1)} %v_ref.13, ...), custom_call_target="tpu_custom_call", output_to_operand_aliasing={{0}: (7, {})} | custom-call | flops 6039797760 | bytes 11796480 | tf_op jit(solution)/shard_map/pallas_call | solution.py:210
  155.5 0.0 collective-permute-done.6.farb_ref
  155.5 0.0 copy-start.1
  155.5 10.1 %shard_map.64 = (bf16[32,10,128,256]{3,2,1,0:T(8,128)(2,1)}, f32[10,32,128]{2,1,0:T(8,128)S(1)}) custom-call(s32[64]{0:T(128)} %pad_add_fusion.s_hbm, bf16[32,10,128,256]{3,2,1,0:T(8,128)(2,1)} %bitcast.6, bf16[32,128,256]{2,1,0:T(8,128)(2,1)} %k_ref.13, bf16[32,128,256]{2,1,0:T(8,128)(2,1)} %v_ref.13, ...), custom_call_target="tpu_custom_call", output_to_operand_aliasing={{0}: (7, {})} | custom-call | flops 3355443200 | bytes 6553600 | tf_op jit(solution)/shard_map/pallas_call | solution.py:210
  165.7 0.0 collective-permute-done.4.farb_ref
  165.7 0.0 copy-done.1
  165.7 5.6 %shard_map.65 = (bf16[32,10,128,256]{3,2,1,0:T(8,128)(2,1)}, f32[10,32,128]{2,1,0:T(8,128)}) custom-call(s32[64]{0:T(128)} %pad_add_fusion.s_hbm, bf16[32,10,128,256]{3,2,1,0:T(8,128)(2,1)} %bitcast.7, bf16[32,128,256]{2,1,0:T(8,128)(2,1)} %k_ref.13, bf16[32,128,256]{2,1,0:T(8,128)(2,1)} %v_ref.13, ...), custom_call_target="tpu_custom_call", output_to_operand_aliasing={{0}: (7, {})} | custom-call | flops 1342177280 | bytes 2621440 | tf_op jit(solution)/shard_map/pallas_call | solution.py:210
  (1 shorter events, 0.0 us)
Async XLA Ops:
  6.6 8.2 %copy-start.2 = (bf16[512,256]{1,0:T(8,128)(2,1)S(1)}, bf16[512,256]{1,0:T(8,128)(2,1)}, u32[]{:S(2)}) copy-start(bf16[512,256]{1,0:T(8,128)(2,1)} %get-tuple-element.18) | copy-start | bytes 786436
  6.6 104.6 %collective-permute-start = (bf16[8224,256]{1,0:T(8,128)(2,1)}, bf16[8224,256]{1,0:T(8,128)(2,1)}, u32[]{:S(2)}, u32[]{:S(2)}) collective-permute-start(bf16[8224,256]{1,0:T(8,128)(2,1)} %get-tuple-element.17), channel_id=1, source_target_pairs={{0,1},{2,3},{4,5},{6,7}} | collective-permute-start | bytes 12632072 | tf_op jit(solution)/shard_map/ppermute | solution.py:240
  8.0 78.9 %collective-permute-start.9 = (bf16[2560,256]{1,0:T(8,128)(2,1)}, bf16[2560,256]{1,0:T(8,128)(2,1)S(1)}, u32[]{:S(2)}, u32[]{:S(2)}) collective-permute-start(bf16[2560,256]{1,0:T(8,128)(2,1)} %get-tuple-element.21), channel_id=1, source_target_pairs={{0,2},{1,3},{4,6},{5,7}} | collective-permute-start | bytes 3932168 | tf_op jit(solution)/shard_map/ppermute | solution.py:240
  12.1 42.4 %collective-permute-start.1 = (bf16[1568,256]{1,0:T(8,128)(2,1)}, bf16[1568,256]{1,0:T(8,128)(2,1)S(1)}, u32[]{:S(2)}, u32[]{:S(2)}) collective-permute-start(bf16[1568,256]{1,0:T(8,128)(2,1)} %shard_map.60), channel_id=1, source_target_pairs={{0,2},{1,3},{4,6},{5,7}} | collective-permute-start | bytes 2408456 | tf_op jit(solution)/shard_map/ppermute | solution.py:240
  13.4 93.4 %collective-permute-start.7 = (bf16[2304,256]{1,0:T(8,128)(2,1)}, bf16[2304,256]{1,0:T(8,128)(2,1)}, u32[]{:S(2)}, u32[]{:S(2)}) collective-permute-start(bf16[2304,256]{1,0:T(8,128)(2,1)} %get-tuple-element.20), channel_id=1, source_target_pairs={{0,2},{1,3},{4,6},{5,7}} | collective-permute-start | bytes 3538952 | tf_op jit(solution)/shard_map/ppermute | solution.py:240
  14.8 70.8 %collective-permute-start.3 = (bf16[512,256]{1,0:T(8,128)(2,1)S(1)}, bf16[512,256]{1,0:T(8,128)(2,1)S(1)}, u32[]{:S(2)}, u32[]{:S(2)}) collective-permute-start(bf16[512,256]{1,0:T(8,128)(2,1)S(1)} %copy-done.2), channel_id=1, source_target_pairs={{0,2},{1,3},{4,6},{5,7}} | collective-permute-start | bytes 786440 | tf_op jit(solution)/shard_map/ppermute | solution.py:240
  54.6 54.2 %collective-permute-start.2 = (bf16[1568,256]{1,0:T(8,128)(2,1)S(1)}, bf16[1568,256]{1,0:T(8,128)(2,1)}, u32[]{:S(2)}, u32[]{:S(2)}) collective-permute-start(bf16[1568,256]{1,0:T(8,128)(2,1)S(1)} %collective-permute-done.1.fara_ref), channel_id=1, source_target_pairs={{2,3},{3,2},{6,7},{7,6}} | collective-permute-start | bytes 2408456 | tf_op jit(solution)/shard_map/ppermute | solution.py:240
  85.6 1.3 copy-start
  85.6 14.7 %collective-permute-start.5 = (bf16[1280,256]{1,0:T(8,128)(2,1)}, bf16[1280,256]{1,0:T(8,128)(2,1)}, u32[]{:S(2)}, u32[]{:S(2)}) collective-permute-start(bf16[1280,256]{1,0:T(8,128)(2,1)} %get-tuple-element.19), channel_id=1, source_target_pairs={{0,2},{1,3},{4,6},{5,7}} | collective-permute-start | bytes 1966088 | tf_op jit(solution)/shard_map/ppermute | solution.py:240
  86.9 37.2 %collective-permute-start.10 = (bf16[2560,256]{1,0:T(8,128)(2,1)S(1)}, bf16[2560,256]{1,0:T(8,128)(2,1)S(1)}, u32[]{:S(2)}, u32[]{:S(2)}) collective-permute-start(bf16[2560,256]{1,0:T(8,128)(2,1)S(1)} %collective-permute-done.9.fara_ref), channel_id=1, source_target_pairs={{2,3},{3,2},{6,7},{7,6}} | collective-permute-start | bytes 3932168 | tf_op jit(solution)/shard_map/ppermute | solution.py:240
  100.3 65.4 %collective-permute-start.4 = (bf16[512,256]{1,0:T(8,128)(2,1)}, bf16[512,256]{1,0:T(8,128)(2,1)S(1)}, u32[]{:S(2)}, u32[]{:S(2)}) collective-permute-start(bf16[512,256]{1,0:T(8,128)(2,1)} %copy-done), channel_id=1, source_target_pairs={{2,3},{3,2},{6,7},{7,6}} | collective-permute-start | bytes 786440 | tf_op jit(solution)/shard_map/ppermute | solution.py:240
  106.9 48.7 %collective-permute-start.6 = (bf16[1280,256]{1,0:T(8,128)(2,1)}, bf16[1280,256]{1,0:T(8,128)(2,1)S(1)}, u32[]{:S(2)}, u32[]{:S(2)}) collective-permute-start(bf16[1280,256]{1,0:T(8,128)(2,1)} %collective-permute-done.5.fara_ref), channel_id=1, source_target_pairs={{2,3},{3,2},{6,7},{7,6}} | collective-permute-start | bytes 1966088 | tf_op jit(solution)/shard_map/ppermute | solution.py:240
  108.8 31.1 %collective-permute-start.8 = (bf16[2304,256]{1,0:T(8,128)(2,1)}, bf16[2304,256]{1,0:T(8,128)(2,1)S(1)}, u32[]{:S(2)}, u32[]{:S(2)}) collective-permute-start(bf16[2304,256]{1,0:T(8,128)(2,1)} %collective-permute-done.7.fara_ref), channel_id=1, source_target_pairs={{2,3},{3,2},{6,7},{7,6}} | collective-permute-start | bytes 3538952 | tf_op jit(solution)/shard_map/ppermute | solution.py:240
  155.5 10.1 %copy-start.1 = (bf16[512,256]{1,0:T(8,128)(2,1)S(1)}, bf16[512,256]{1,0:T(8,128)(2,1)}, u32[]{:S(2)}) copy-start(bf16[512,256]{1,0:T(8,128)(2,1)} %copy-done) | copy-start | bytes 786436
where the time goes:
time: 172 us; the launch traced here: 171 us
  waiting for transfers between devices  67.8 us (39%)
  Pallas kernels  67.3 us (39%)
  starting transfers between devices  33.9 us (20%)
    ppermute x11, waiting for transfers between devices, shift(): return lax.ppermute(x, 'cp', pairs)  67.8 us
    pallas_call x5, Pallas kernels, attend(): pl.pallas_call(functools.partial(attend_kernel, first, base, size), in_sp...  58.5 us
    ppermute x11, starting transfers between devices, shift(): return lax.ppermute(x, 'cp', pairs)  33.9 us
    pallas_call x2, Pallas kernels, pack(): pl.pallas_call(functools.partial(pack_kernel, ranges, tails), in_specs=[p...  8.76 us
  transfers between devices with their start and end apart: 11, of which 3 were waited for; matrix products, arithmetic and copies ran while one was open for 1% of the time, Pallas kernels for 33%

commit v1 on v0

--- a/solution.py
+++ b/solution.py
@@ -8,7 +8,7 @@
 from jax.sharding import PartitionSpec as P
 
 
-CHUNKS = (6, 10, 9, 5, 2)
+CHUNKS = (6, 6, 5, 5, 5, 5)
 BOUNDS = tuple(sum(CHUNKS[:n]) for n in range(len(CHUNKS) + 1))
 GROUP = 2
 DEPTH = 3
@@ -77,6 +77,7 @@
         _, lse_in, o_ref, lse_ref, *scratch = rest
     s_ref, q_buf, k_buf, v_buf, o_buf, s_sem, kv_sem, q_sem, o_sem = scratch
     depth, heads, piece, head = q_buf.shape
+    batch = lse_ref.shape[1]
     groups = heads // GROUP
     width = GROUP * piece
     scale = head ** -0.5
@@ -184,7 +185,11 @@
                 o_store(step - 2, g).wait()
 
         place(step)
-        run(4, step, s_ref[base + step])
+        cut, need = s_ref[base + step], s_ref[batch + base + step]
+        for count in (2, 3, 4):
+            @pl.when((need == count) | (count == 2 and need == 1))
+            def _():
+                run(count, step, cut)
         for g in range(groups):
             o_store(step, g).start()
 

time: 172 us -> 172 us (level)
  starting transfers between devices: 33.9 us -> 39.8 us
  Pallas kernels: 67.3 us -> 62.4 us
  waiting for transfers between devices: 67.8 us -> 65.1 us
    ppermute x11 -> x13, starting transfers between devices: 33.9 us -> 39.8 us  [shift(): return lax.ppermute(x, 'cp', pairs)]
    pallas_call x5 -> x6, Pallas kernels: 58.5 us -> 53.6 us  [attend(): pl.pallas_call(functools.partial(attend_kernel, first, base, size), in_sp...]
    ppermute x11 -> x13, waiting for transfers between devices: 67.8 us -> 65.1 us  [shift(): return lax.ppermute(x, 'cp', pairs)]
  transfers between devices with their start and end apart: 11 -> 13, of which waited for: 3 -> 5; matrix products, arithmetic and copies ran while one was open for 1% -> 1% of each run, Pallas kernels for 33% -> 28%
where the time goes in v1:
time: 172 us; the launch traced here: 170 us
  waiting for transfers between devices  65.1 us (38%)
  Pallas kernels  62.4 us (36%)
  starting transfers between devices  39.8 us (23%)
    ppermute x13, waiting for transfers between devices, shift(): return lax.ppermute(x, 'cp', pairs)  65.1 us
    pallas_call x6, Pallas kernels, attend(): pl.pallas_call(functools.partial(attend_kernel, first, base, size), in_sp...  53.6 us
    ppermute x13, starting transfers between devices, shift(): return lax.ppermute(x, 'cp', pairs)  39.8 us
    pallas_call x2, Pallas kernels, pack(): pl.pallas_call(functools.partial(pack_kernel, ranges, tails), in_specs=[p...  8.77 us
  transfers between devices with their start and end apart: 13, of which 5 were waited for; matrix products, arithmetic and copies ran while one was open for 1% of the time, Pallas kernels for 28%

profile of v1, /device:TPU:7, one launch (start us, length us, event | category | flops | bytes accessed | tf_op | source)
XLA Modules:
  0.0 169.8 jit_solution(6727925084608297885)
XLA Ops:
  0.6 5.9 %shard_map.59 = (bf16[1536,256]{1,0:T(8,128)(2,1)}, bf16[1280,256]{1,0:T(8,128)(2,1)}, bf16[1280,256]{1,0:T(8,128)(2,1)}, bf16[1280,256]{1,0:T(8,128)(2,1)}, bf1...) custom-call(s32[32,128]{1,0:T(8,128)} %seg_ref.3, bf16[32,128,256]{2,1,0:T(8,128)(2,1)} %k_ref.15, ...), custom_call_target="tpu_custom_call" | custom-call | flops 1048576 | bytes 4194304 | tf_op jit(solution)/shard_map/pallas_call | solution.py:54
  6.6 1.3 collective-permute-start
  7.9 2.8 %shard_map.60 = bf16[1568,256]{1,0:T(8,128)(2,1)} custom-call(s32[32,128]{1,0:T(8,128)} %seg_ref.3, bf16[32,128,256]{2,1,0:T(8,128)(2,1)} %k_ref.15, bf16[32,128,256]{2,1,0:T(8,128)(2,1)} %v_ref.15), custom_call_target="tpu_custom_call" | custom-call | flops 1048576 | bytes 4194304 | tf_op jit(solution)/shard_map/pallas_call | solution.py:54
  10.7 1.3 collective-permute-start.1
  12.0 1.3 collective-permute-start.9
  13.3 1.3 collective-permute-start.7
  14.6 14.6 %collective-permute-done.1.fara_ref = bf16[1568,256]{1,0:T(8,128)(2,1)S(1)} collective-permute-done((bf16[1568,256]{1,0:T(8,128)(2,1)}, bf16[1568,256]{1,0:T(8,128)(2,1)S(1)}, u32[]{:S(2)}, u32[]{:S(2)}) %collective-permute-start.1) | collective-permute-done | bytes 802848 | tf_op jit(solution)/shard_map/ppermute | solution.py:245
  29.2 9.4 %collective-permute-start.2 = (bf16[1568,256]{1,0:T(8,128)(2,1)S(1)}, bf16[1568,256]{1,0:T(8,128)(2,1)S(1)}, u32[]{:S(2)}, u32[]{:S(2)}) collective-permute-start(bf16[1568,256]{1,0:T(8,128)(2,1)S(1)} %collective-permute-done.1.fara_ref), channel_id=1, source_target_pairs={{2,3},{3,2},{6,7},{7,6}} | collective-permute-start | bytes 2408456 | tf_op jit(solution)/shard_map/ppermute | solution.py:245
  38.6 1.3 collective-permute-start.11
  39.9 3.4 %collective-permute-done.9.fara_ref = bf16[1280,256]{1,0:T(8,128)(2,1)S(1)} collective-permute-done((bf16[1280,256]{1,0:T(8,128)(2,1)}, bf16[1280,256]{1,0:T(8,128)(2,1)S(1)}, u32[]{:S(2)}, u32[]{:S(2)}) %collective-permute-start.9) | collective-permute-done | bytes 655392 | tf_op jit(solution)/shard_map/ppermute | solution.py:245
  43.2 0.0 copy-start
  43.2 1.3 collective-permute-start.5
  44.5 12.8 %collective-permute-done.7.fara_ref = bf16[1280,256]{1,0:T(8,128)(2,1)S(1)} collective-permute-done((bf16[1280,256]{1,0:T(8,128)(2,1)}, bf16[1280,256]{1,0:T(8,128)(2,1)S(1)}, u32[]{:S(2)}, u32[]{:S(2)}) %collective-permute-start.7) | collective-permute-done | bytes 655392 | tf_op jit(solution)/shard_map/ppermute | solution.py:245
  57.3 0.0 copy-done
  57.3 1.3 collective-permute-start.3
  58.6 29.7 %collective-permute-done.5.fara_ref = bf16[1280,256]{1,0:T(8,128)(2,1)} collective-permute-done((bf16[1280,256]{1,0:T(8,128)(2,1)}, bf16[1280,256]{1,0:T(8,128)(2,1)}, u32[]{:S(2)}, u32[]{:S(2)}) %collective-permute-start.5) | collective-permute-done | bytes 655392 | tf_op jit(solution)/shard_map/ppermute | solution.py:245
  88.3 9.4 %collective-permute-start.10 = (bf16[1280,256]{1,0:T(8,128)(2,1)}, bf16[1280,256]{1,0:T(8,128)(2,1)S(1)}, u32[]{:S(2)}, u32[]{:S(2)}) collective-permute-start(bf16[1280,256]{1,0:T(8,128)(2,1)} %copy-done), channel_id=1, source_target_pairs={{2,3},{3,2},{6,7},{7,6}} | collective-permute-start | bytes 1966088 | tf_op jit(solution)/shard_map/ppermute | solution.py:245
  97.6 4.7 %collective-permute-done.3.fara_ref = bf16[1280,256]{1,0:T(8,128)(2,1)} collective-permute-done((bf16[1280,256]{1,0:T(8,128)(2,1)}, bf16[1280,256]{1,0:T(8,128)(2,1)}, u32[]{:S(2)}, u32[]{:S(2)}) %collective-permute-start.3) | collective-permute-done | bytes 655392 | tf_op jit(solution)/shard_map/ppermute | solution.py:245
  102.3 5.8 %collective-permute-start.8 = (bf16[1280,256]{1,0:T(8,128)(2,1)S(1)}, bf16[1280,256]{1,0:T(8,128)(2,1)S(1)}, u32[]{:S(2)}, u32[]{:S(2)}) collective-permute-start(bf16[1280,256]{1,0:T(8,128)(2,1)S(1)} %collective-permute-done.7.fara_ref), channel_id=1, source_target_pairs={{2,3},{3,2},{6,7},{7,6}} | collective-permute-start | bytes 1966088 | tf_op jit(solution)/shard_map/ppermute | solution.py:245
  108.2 0.0 collective-permute-done.11.fara_ref
  108.2 1.9 %collective-permute-start.6 = (bf16[1280,256]{1,0:T(8,128)(2,1)}, bf16[1280,256]{1,0:T(8,128)(2,1)S(1)}, u32[]{:S(2)}, u32[]{:S(2)}) collective-permute-start(bf16[1280,256]{1,0:T(8,128)(2,1)} %collective-permute-done.5.fara_ref), channel_id=1, source_target_pairs={{2,3},{3,2},{6,7},{7,6}} | collective-permute-start | bytes 1966088 | tf_op jit(solution)/shard_map/ppermute | solution.py:245
  110.1 0.0 collective-permute-done.2.farb_ref
  110.1 2.4 %collective-permute-start.4 = (bf16[1280,256]{1,0:T(8,128)(2,1)}, bf16[1280,256]{1,0:T(8,128)(2,1)S(1)}, u32[]{:S(2)}, u32[]{:S(2)}) collective-permute-start(bf16[1280,256]{1,0:T(8,128)(2,1)} %collective-permute-done.3.fara_ref), channel_id=1, source_target_pairs={{2,3},{3,2},{6,7},{7,6}} | collective-permute-start | bytes 1966088 | tf_op jit(solution)/shard_map/ppermute | solution.py:245
  112.5 0.0 collective-permute-done.near_ref
  112.5 1.9 %collective-permute-start.12 = (bf16[1536,256]{1,0:T(8,128)(2,1)S(1)}, bf16[1536,256]{1,0:T(8,128)(2,1)S(1)}, u32[]{:S(2)}, u32[]{:S(2)}) collective-permute-start(bf16[1536,256]{1,0:T(8,128)(2,1)S(1)} %collective-permute-done.11.fara_ref), channel_id=1, source_target_pairs={{2,3},{3,2},{6,7},{7,6}} | collective-permute-start | bytes 2359304 | tf_op jit(solution)/shard_map/ppermute | solution.py:245
  114.5 0.8 add_reduce_fusion
  115.3 0.7 pad_add_fusion.s_hbm
  116.0 9.8 %shard_map.61 = (bf16[32,10,128,256]{3,2,1,0:T(8,128)(2,1)}, f32[10,32,128]{2,1,0:T(8,128)S(1)}) custom-call(s32[64]{0:T(128)} %pad_add_fusion.s_hbm, bf16[32,10,128,256]{3,2,1,0:T(8,128)(2,1)} %bitcast.3, bf16[32,128,256]{2,1,0:T(8,128)(2,1)} %k_ref.15, bf16[32,128,256]{2,1,0:T(8,128)(2,1)} %v_ref.15, bf16[8224,256]{1,0:T(8,128)(2,1)} %collective-permute-done.near_ref, ...), custom_call_target="tpu_custom_call" | custom-call | flops 4026531840 | bytes 7864320 | tf_op jit(solution)/shard_map/pallas_call | solution.py:215
  125.8 0.0 collective-permute-done.12.farb_ref
  125.8 0.0 copy-start.1
  125.8 10.1 %shard_map.62 = (bf16[32,10,128,256]{3,2,1,0:T(8,128)(2,1)}, f32[10,32,128]{2,1,0:T(8,128)S(1)}) custom-call(s32[64]{0:T(128)} %pad_add_fusion.s_hbm, bf16[32,10,128,256]{3,2,1,0:T(8,128)(2,1)} %bitcast.4, bf16[32,128,256]{2,1,0:T(8,128)(2,1)} %k_ref.15, bf16[32,128,256]{2,1,0:T(8,128)(2,1)} %v_ref.15, ...), custom_call_target="tpu_custom_call", output_to_operand_aliasing={{0}: (7, {})} | custom-call | flops 4026531840 | bytes 7864320 | tf_op jit(solution)/shard_map/pallas_call | solution.py:215
  135.9 0.0 collective-permute-done.10.farb_ref
  135.9 0.0 copy-done.1
  135.9 7.6 %shard_map.63 = (bf16[32,10,128,256]{3,2,1,0:T(8,128)(2,1)}, f32[10,32,128]{2,1,0:T(8,128)S(1)}) custom-call(s32[64]{0:T(128)} %pad_add_fusion.s_hbm, bf16[32,10,128,256]{3,2,1,0:T(8,128)(2,1)} %bitcast.5, bf16[32,128,256]{2,1,0:T(8,128)(2,1)} %k_ref.15, bf16[32,128,256]{2,1,0:T(8,128)(2,1)} %v_ref.15, ...), custom_call_target="tpu_custom_call", output_to_operand_aliasing={{0}: (7, {})} | custom-call | flops 3355443200 | bytes 6553600 | tf_op jit(solution)/shard_map/pallas_call | solution.py:215
  143.6 0.0 collective-permute-done.8.farb_ref
  143.6 8.1 %shard_map.64 = (bf16[32,10,128,256]{3,2,1,0:T(8,128)(2,1)}, f32[10,32,128]{2,1,0:T(8,128)S(1)}) custom-call(s32[64]{0:T(128)} %pad_add_fusion.s_hbm, bf16[32,10,128,256]{3,2,1,0:T(8,128)(2,1)} %bitcast.6, bf16[32,128,256]{2,1,0:T(8,128)(2,1)} %k_ref.15, bf16[32,128,256]{2,1,0:T(8,128)(2,1)} %v_ref.15, ...), custom_call_target="tpu_custom_call", output_to_operand_aliasing={{0}: (7, {})} | custom-call | flops 3355443200 | bytes 6553600 | tf_op jit(solution)/shard_map/pallas_call | solution.py:215
  151.7 0.0 collective-permute-done.6.farb_ref
  151.7 9.2 %shard_map.65 = (bf16[32,10,128,256]{3,2,1,0:T(8,128)(2,1)}, f32[10,32,128]{2,1,0:T(8,128)S(1)}) custom-call(s32[64]{0:T(128)} %pad_add_fusion.s_hbm, bf16[32,10,128,256]{3,2,1,0:T(8,128)(2,1)} %bitcast.7, bf16[32,128,256]{2,1,0:T(8,128)(2,1)} %k_ref.15, bf16[32,128,256]{2,1,0:T(8,128)(2,1)} %v_ref.15, ...), custom_call_target="tpu_custom_call", output_to_operand_aliasing={{0}: (7, {})} | custom-call | flops 3355443200 | bytes 6553600 | tf_op jit(solution)/shard_map/pallas_call | solution.py:215
  160.9 0.0 collective-permute-done.4.farb_ref
  160.9 8.8 %shard_map.66 = (bf16[32,10,128,256]{3,2,1,0:T(8,128)(2,1)}, f32[10,32,128]{2,1,0:T(8,128)}) custom-call(s32[64]{0:T(128)} %pad_add_fusion.s_hbm, bf16[32,10,128,256]{3,2,1,0:T(8,128)(2,1)} %bitcast.8, bf16[32,128,256]{2,1,0:T(8,128)(2,1)} %k_ref.15, bf16[32,128,256]{2,1,0:T(8,128)(2,1)} %v_ref.15, ...), custom_call_target="tpu_custom_call", output_to_operand_aliasing={{0}: (7, {})} | custom-call | flops 3355443200 | bytes 6553600 | tf_op jit(solution)/shard_map/pallas_call | solution.py:215
  (1 shorter events, 0.0 us)
Async XLA Ops:
  6.6 106.0 %collective-permute-start = (bf16[8224,256]{1,0:T(8,128)(2,1)}, bf16[8224,256]{1,0:T(8,128)(2,1)}, u32[]{:S(2)}, u32[]{:S(2)}) collective-permute-start(bf16[8224,256]{1,0:T(8,128)(2,1)} %get-tuple-element.20), channel_id=1, source_target_pairs={{0,1},{2,3},{4,5},{6,7}} | collective-permute-start | bytes 12632072 | tf_op jit(solution)/shard_map/ppermute | solution.py:245
  10.7 18.5 %collective-permute-start.1 = (bf16[1568,256]{1,0:T(8,128)(2,1)}, bf16[1568,256]{1,0:T(8,128)(2,1)S(1)}, u32[]{:S(2)}, u32[]{:S(2)}) collective-permute-start(bf16[1568,256]{1,0:T(8,128)(2,1)} %shard_map.60), channel_id=1, source_target_pairs={{0,2},{1,3},{4,6},{5,7}} | collective-permute-start | bytes 2408456 | tf_op jit(solution)/shard_map/ppermute | solution.py:245
  12.0 31.2 %collective-permute-start.9 = (bf16[1280,256]{1,0:T(8,128)(2,1)}, bf16[1280,256]{1,0:T(8,128)(2,1)S(1)}, u32[]{:S(2)}, u32[]{:S(2)}) collective-permute-start(bf16[1280,256]{1,0:T(8,128)(2,1)} %get-tuple-element.24), channel_id=1, source_target_pairs={{0,2},{1,3},{4,6},{5,7}} | collective-permute-start | bytes 1966088 | tf_op jit(solution)/shard_map/ppermute | solution.py:245
  13.3 44.0 %collective-permute-start.7 = (bf16[1280,256]{1,0:T(8,128)(2,1)}, bf16[1280,256]{1,0:T(8,128)(2,1)S(1)}, u32[]{:S(2)}, u32[]{:S(2)}) collective-permute-start(bf16[1280,256]{1,0:T(8,128)(2,1)} %get-tuple-element.23), channel_id=1, source_target_pairs={{0,2},{1,3},{4,6},{5,7}} | collective-permute-start | bytes 1966088 | tf_op jit(solution)/shard_map/ppermute | solution.py:245
  29.2 80.9 %collective-permute-start.2 = (bf16[1568,256]{1,0:T(8,128)(2,1)S(1)}, bf16[1568,256]{1,0:T(8,128)(2,1)S(1)}, u32[]{:S(2)}, u32[]{:S(2)}) collective-permute-start(bf16[1568,256]{1,0:T(8,128)(2,1)S(1)} %collective-permute-done.1.fara_ref), channel_id=1, source_target_pairs={{2,3},{3,2},{6,7},{7,6}} | collective-permute-start | bytes 2408456 | tf_op jit(solution)/shard_map/ppermute | solution.py:245
  38.6 69.6 %collective-permute-start.11 = (bf16[1536,256]{1,0:T(8,128)(2,1)}, bf16[1536,256]{1,0:T(8,128)(2,1)S(1)}, u32[]{:S(2)}, u32[]{:S(2)}) collective-permute-start(bf16[1536,256]{1,0:T(8,128)(2,1)} %get-tuple-element.25), channel_id=1, source_target_pairs={{0,2},{1,3},{4,6},{5,7}} | collective-permute-start | bytes 2359304 | tf_op jit(solution)/shard_map/ppermute | solution.py:245
  43.2 14.0 %copy-start = (bf16[1280,256]{1,0:T(8,128)(2,1)}, bf16[1280,256]{1,0:T(8,128)(2,1)S(1)}, u32[]{:S(2)}) copy-start(bf16[1280,256]{1,0:T(8,128)(2,1)S(1)} %collective-permute-done.9.fara_ref) | copy-start | bytes 1966084
  43.2 45.0 %collective-permute-start.5 = (bf16[1280,256]{1,0:T(8,128)(2,1)}, bf16[1280,256]{1,0:T(8,128)(2,1)}, u32[]{:S(2)}, u32[]{:S(2)}) collective-permute-start(bf16[1280,256]{1,0:T(8,128)(2,1)} %get-tuple-element.22), channel_id=1, source_target_pairs={{0,2},{1,3},{4,6},{5,7}} | collective-permute-start | bytes 1966088 | tf_op jit(solution)/shard_map/ppermute | solution.py:245
  57.3 45.0 %collective-permute-start.3 = (bf16[1280,256]{1,0:T(8,128)(2,1)}, bf16[1280,256]{1,0:T(8,128)(2,1)}, u32[]{:S(2)}, u32[]{:S(2)}) collective-permute-start(bf16[1280,256]{1,0:T(8,128)(2,1)} %get-tuple-element.21), channel_id=1, source_target_pairs={{0,2},{1,3},{4,6},{5,7}} | collective-permute-start | bytes 1966088 | tf_op jit(solution)/shard_map/ppermute | solution.py:245
  88.3 47.6 %collective-permute-start.10 = (bf16[1280,256]{1,0:T(8,128)(2,1)}, bf16[1280,256]{1,0:T(8,128)(2,1)S(1)}, u32[]{:S(2)}, u32[]{:S(2)}) collective-permute-start(bf16[1280,256]{1,0:T(8,128)(2,1)} %copy-done), channel_id=1, source_target_pairs={{2,3},{3,2},{6,7},{7,6}} | collective-permute-start | bytes 1966088 | tf_op jit(solution)/shard_map/ppermute | solution.py:245
  102.3 41.2 %collective-permute-start.8 = (bf16[1280,256]{1,0:T(8,128)(2,1)S(1)}, bf16[1280,256]{1,0:T(8,128)(2,1)S(1)}, u32[]{:S(2)}, u32[]{:S(2)}) collective-permute-start(bf16[1280,256]{1,0:T(8,128)(2,1)S(1)} %collective-permute-done.7.fara_ref), channel_id=1, source_target_pairs={{2,3},{3,2},{6,7},{7,6}} | collective-permute-start | bytes 1966088 | tf_op jit(solution)/shard_map/ppermute | solution.py:245
  108.2 43.5 %collective-permute-start.6 = (bf16[1280,256]{1,0:T(8,128)(2,1)}, bf16[1280,256]{1,0:T(8,128)(2,1)S(1)}, u32[]{:S(2)}, u32[]{:S(2)}) collective-permute-start(bf16[1280,256]{1,0:T(8,128)(2,1)} %collective-permute-done.5.fara_ref), channel_id=1, source_target_pairs={{2,3},{3,2},{6,7},{7,6}} | collective-permute-start | bytes 1966088 | tf_op jit(solution)/shard_map/ppermute | solution.py:245
  110.1 50.7 %collective-permute-start.4 = (bf16[1280,256]{1,0:T(8,128)(2,1)}, bf16[1280,256]{1,0:T(8,128)(2,1)S(1)}, u32[]{:S(2)}, u32[]{:S(2)}) collective-permute-start(bf16[1280,256]{1,0:T(8,128)(2,1)} %collective-permute-done.3.fara_ref), channel_id=1, source_target_pairs={{2,3},{3,2},{6,7},{7,6}} | collective-permute-start | bytes 1966088 | tf_op jit(solution)/shard_map/ppermute | solution.py:245
  112.5 13.2 %collective-permute-start.12 = (bf16[1536,256]{1,0:T(8,128)(2,1)S(1)}, bf16[1536,256]{1,0:T(8,128)(2,1)S(1)}, u32[]{:S(2)}, u32[]{:S(2)}) collective-permute-start(bf16[1536,256]{1,0:T(8,128)(2,1)S(1)} %collective-permute-done.11.fara_ref), channel_id=1, source_target_pairs={{2,3},{3,2},{6,7},{7,6}} | collective-permute-start | bytes 2359304 | tf_op jit(solution)/shard_map/ppermute | solution.py:245
  125.8 10.2 %copy-start.1 = (bf16[1280,256]{1,0:T(8,128)(2,1)S(1)}, bf16[1280,256]{1,0:T(8,128)(2,1)}, u32[]{:S(2)}) copy-start(bf16[1280,256]{1,0:T(8,128)(2,1)} %copy-done) | copy-start | bytes 1966084

commit v2 on v1

--- a/solution.py
+++ b/solution.py
@@ -70,12 +70,13 @@
     )(seg, k, v)
 
 
-def attend_kernel(first, base, size, s_hbm, q_ref, k_ref, v_ref, near_ref, fara_ref, farb_ref, *rest):
-    if first:
-        o_ref, lse_ref, *scratch = rest
-    else:
-        _, lse_in, o_ref, lse_ref, *scratch = rest
-    s_ref, q_buf, k_buf, v_buf, o_buf, s_sem, kv_sem, q_sem, o_sem = scratch
+def attend_kernel(first, last, base, size, s_hbm, cut_ref, q_ref, k_ref, v_ref, near_ref, fara_ref, farb_ref, *rest):
+    if not first:
+        _, lse_in, q_in, kv_in, *rest = rest
+    o_ref, lse_ref, *rest = rest
+    if not last:
+        q_out, kv_out, *rest = rest
+    s_ref, n_ref, q_buf, k_buf, v_buf, o_buf, s_sem, kv_sem, q_sem, o_sem, ahead_sem = rest
     depth, heads, piece, head = q_buf.shape
     batch = lse_ref.shape[1]
     groups = heads // GROUP
@@ -95,6 +96,15 @@
             rows = pl.ds(pl.multiple_of((2 * seq + half) * piece, piece), piece)
             out.append(pltpu.make_async_copy(ref.at[seq], buf.at[slot, pl.ds(0, piece)], kv_sem.at[slot]))
             out.append(pltpu.make_async_copy(near_ref.at[rows], buf.at[slot, there], kv_sem.at[slot]))
+        return out
+
+    def aheads():
+        at = base + size
+        out = [pltpu.make_async_copy(q_ref.at[at], q_out, ahead_sem)]
+        for half, ref in enumerate((k_ref, v_ref)):
+            near_rows = pl.ds((2 * at + half) * piece, piece)
+            out.append(pltpu.make_async_copy(ref.at[at], kv_out.at[2 * half], ahead_sem))
+            out.append(pltpu.make_async_copy(near_ref.at[near_rows], kv_out.at[2 * half + 1], ahead_sem))
         return out
 
     def part(g):
@@ -147,6 +157,7 @@
         def finish(g, logs, p, m, l):
             o = jnp.dot(p, v_buf[slot, :keys], preferred_element_type=jnp.float32) * (1.0 / l)
             o_buf[out, g * GROUP:(g + 1) * GROUP] = o.astype(jnp.bfloat16).reshape(GROUP, piece, head)
+            o_store(step, g).start()
             e = m * scale + jnp.log(l)
             for j in range(GROUP):
                 logs = jnp.where(lane == g * GROUP + j, e[j * piece:(j + 1) * piece], logs)
@@ -161,23 +172,39 @@
         logs = finish(groups - 1, logs, *before)
         lse_ref[:, pl.ds(seq, 1), :] = logs.T[:heads][:, None, :]
 
-    load(0)
-    if size > 1:
-        load(1)
-    if not first:
+    n_ref[0] = jnp.where(me >= 2, 4, 2)
+    if first:
+        load(0)
+    else:
+        q_buf[0] = q_in[...]
+        there = pl.ds(pl.multiple_of(jnp.where(odd == 1, 1, 3) * piece, piece), piece)
+        for half, buf in enumerate((k_buf, v_buf)):
+            buf[0, :piece] = kv_in[2 * half]
+            buf[0, there] = kv_in[2 * half + 1]
         lse_ref[...] = lse_in[...]
-    scalars.wait()
 
     @pl.loop(0, size)
     def _(step):
-        for copy in kv_loads(step):
-            copy.wait()
-        for g in range(groups):
-            q_load(step, g).wait()
+        @pl.when((step > 0) | first)
+        def _():
+            for copy in kv_loads(step):
+                copy.wait()
+            for g in range(groups):
+                q_load(step, g).wait()
+
+        @pl.when((step == 0) & (size > 1))
+        def _():
+            load(1)
 
         @pl.when(step + 2 < size)
         def _():
             load(step + 2)
+
+        if not last:
+            @pl.when(step == max(size - 2, 0))
+            def _():
+                for copy in aheads():
+                    copy.start()
 
         @pl.when(step >= 2)
         def _():
@@ -185,39 +212,56 @@
                 o_store(step - 2, g).wait()
 
         place(step)
-        cut, need = s_ref[base + step], s_ref[batch + base + step]
+        need = n_ref[0]
         for count in (2, 3, 4):
             @pl.when((need == count) | (count == 2 and need == 1))
             def _():
-                run(count, step, cut)
-        for g in range(groups):
-            o_store(step, g).start()
-
+                run(count, step, cut_ref[pl.ds(base + step, 1), :])
+
+        @pl.when(step == 0)
+        def _():
+            scalars.wait()
+
+        n_ref[0] = s_ref[jnp.minimum(base + step + 1, batch - 1)]
+
+    if not last:
+        for copy in aheads():
+            copy.wait()
     for step in range(max(size - 2, 0), size):
         for g in range(groups):
             o_store(step, g).wait()
 
 
-def attend(n, scalars, q, k, v, near, fara, farb, prev):
+def attend(n, needs, cuts, q, k, v, near, fara, farb, prev):
     batch, heads, piece, head = q.shape
     base, size = BOUNDS[n], CHUNKS[n]
-    first = prev is None
+    first, last = prev is None, n == len(CHUNKS) - 1
     hbm = pl.BlockSpec(memory_space=pltpu.HBM)
     vmem = pl.BlockSpec(memory_space=pltpu.VMEM)
-    in_specs = [hbm] * 5 + [vmem] * 2
-    scalars, q, k, v, near = (pltpu.with_memory_space_constraint(x, pltpu.HBM) for x in (scalars, q, k, v, near))
-    args = [scalars, q, k, v, near, fara, farb]
+    in_specs = [hbm, vmem] + [hbm] * 4 + [vmem] * 2
+    needs, q, k, v, near = (pltpu.with_memory_space_constraint(x, pltpu.HBM) for x in (needs, q, k, v, near))
+    args = [needs, cuts, q, k, v, near, fara, farb]
     aliases = {}
     if not first:
-        in_specs += [hbm, vmem]
+        in_specs += [hbm, vmem, vmem, vmem]
         args += list(prev)
-        aliases = {7: 0}
+        aliases = {8: 0}
+    out_shape = [
+        jax.ShapeDtypeStruct(q.shape, jnp.bfloat16),
+        jax.ShapeDtypeStruct((heads, batch, piece), jnp.float32),
+    ]
+    if not last:
+        out_shape += [
+            jax.ShapeDtypeStruct(q.shape[1:], jnp.bfloat16),
+            jax.ShapeDtypeStruct((4, piece, head), jnp.bfloat16),
+        ]
     return pl.pallas_call(
-        functools.partial(attend_kernel, first, base, size),
+        functools.partial(attend_kernel, first, last, base, size),
         in_specs=in_specs,
-        out_specs=[hbm, vmem],
+        out_specs=[hbm] + [vmem] * (len(out_shape) - 1),
         scratch_shapes=[
-            pltpu.SMEM(scalars.shape, jnp.int32),
+            pltpu.SMEM(needs.shape, jnp.int32),
+            pltpu.SMEM((1,), jnp.int32),
             pltpu.VMEM((DEPTH, heads, piece, head), jnp.bfloat16),
             pltpu.VMEM((DEPTH, 4 * piece, head), jnp.bfloat16),
             pltpu.VMEM((DEPTH, 4 * piece, head), jnp.bfloat16),
@@ -226,11 +270,9 @@
             pltpu.SemaphoreType.DMA((DEPTH,)),
             pltpu.SemaphoreType.DMA((DEPTH, heads // GROUP)),
             pltpu.SemaphoreType.DMA((2, heads // GROUP)),
+            pltpu.SemaphoreType.DMA,
         ],
-        out_shape=[
-            jax.ShapeDtypeStruct(q.shape, jnp.bfloat16),
-            jax.ShapeDtypeStruct((heads, batch, piece), jnp.float32),
-        ],
+        out_shape=out_shape,
         input_output_aliases=aliases,
         compiler_params=pltpu.CompilerParams(vmem_limit_bytes=32 << 20),
         cost_estimate=pl.CostEstimate(
@@ -264,11 +306,11 @@
         odd, upper = me % 2 == 1, me >= 2
         cuts = zeros(whole, True) + zeros(near, odd) + zeros(fara[0], upper) + zeros(farb[0], upper)
         need = jnp.where(cuts <= me * piece, me - cuts // piece, me) + 1
-        scalars = jnp.concatenate([cuts - me * piece, need.astype(jnp.int32)])
+        table = jnp.broadcast_to((cuts - me * piece)[:, None], (batch, piece))
         state = None
         for n in range(len(CHUNKS)):
-            state = attend(n, scalars, q, k_loc, v_loc, near, fara[n], farb[n], state)
-        out, lse = state
+            state = attend(n, need.astype(jnp.int32), table, q, k_loc, v_loc, near, fara[n], farb[n], state)
+        out, lse = state[:2]
         return jnp.transpose(out, (0, 2, 1, 3)), jnp.transpose(lse, (1, 2, 0))
 
     return jax.shard_map(

time: 172 us -> 164 us (0.953)
  waiting for transfers between devices: 65.1 us -> 55.7 us
  starting transfers between devices: 39.8 us -> 47.3 us
  Pallas kernels: 62.4 us -> 57.5 us
    ppermute x13, waiting for transfers between devices: 65.1 us -> 55.7 us  [shift(): return lax.ppermute(x, 'cp', pairs)]
    ppermute x13, starting transfers between devices: 39.8 us -> 47.3 us  [shift(): return lax.ppermute(x, 'cp', pairs)]
    pallas_call x6, Pallas kernels: 53.6 us -> 48.7 us  [attend(): pl.pallas_call(functools.partial(attend_kernel, first, last, base, size),...]
  transfers between devices with their start and end apart: 13 -> 13, of which waited for: 5 -> 6; matrix products, arithmetic and copies ran while one was open for 1% -> 1% of each run, Pallas kernels for 28% -> 27%
where the time goes in v2:
time: 164 us; the launch traced here: 163 us
  Pallas kernels  57.5 us (35%)
  waiting for transfers between devices  55.7 us (34%)
  starting transfers between devices  47.3 us (29%)
    ppermute x13, waiting for transfers between devices, shift(): return lax.ppermute(x, 'cp', pairs)  55.7 us
    pallas_call x6, Pallas kernels, attend(): pl.pallas_call(functools.partial(attend_kernel, first, last, base, size),...  48.7 us
    ppermute x13, starting transfers between devices, shift(): return lax.ppermute(x, 'cp', pairs)  47.3 us
    pallas_call x2, Pallas kernels, pack(): pl.pallas_call(functools.partial(pack_kernel, ranges, tails), in_specs=[p...  8.78 us
  transfers between devices with their start and end apart: 13, of which 6 were waited for; matrix products, arithmetic and copies ran while one was open for 1% of the time, Pallas kernels for 27%

profile of v2, /device:TPU:7, one launch (start us, length us, event | category | flops | bytes accessed | tf_op | source)
XLA Modules:
  0.0 163.0 jit_solution(481765101887817626)
XLA Ops:
  0.6 5.9 %shard_map.59 = (bf16[1536,256]{1,0:T(8,128)(2,1)}, bf16[1280,256]{1,0:T(8,128)(2,1)}, bf16[1280,256]{1,0:T(8,128)(2,1)}, bf16[1280,256]{1,0:T(8,128)(2,1)}, bf1...) custom-call(s32[32,128]{1,0:T(8,128)} %seg_ref.3, bf16[32,128,256]{2,1,0:T(8,128)(2,1)} %k_ref.15, ...), custom_call_target="tpu_custom_call" | custom-call | flops 1048576 | bytes 4194304 | tf_op jit(solution)/shard_map/pallas_call | solution.py:54
  6.6 1.3 collective-permute-start
  7.9 2.8 %shard_map.60 = bf16[1568,256]{1,0:T(8,128)(2,1)} custom-call(s32[32,128]{1,0:T(8,128)} %seg_ref.3, bf16[32,128,256]{2,1,0:T(8,128)(2,1)} %k_ref.15, bf16[32,128,256]{2,1,0:T(8,128)(2,1)} %v_ref.15), custom_call_target="tpu_custom_call" | custom-call | flops 1048576 | bytes 4194304 | tf_op jit(solution)/shard_map/pallas_call | solution.py:54
  10.7 1.3 collective-permute-start.1
  12.0 1.3 collective-permute-start.9
  13.3 1.3 collective-permute-start.7
  14.6 1.3 collective-permute-start.11
  15.9 13.3 %collective-permute-done.1.fara_ref = bf16[1568,256]{1,0:T(8,128)(2,1)S(1)} collective-permute-done((bf16[1568,256]{1,0:T(8,128)(2,1)}, bf16[1568,256]{1,0:T(8,128)(2,1)S(1)}, u32[]{:S(2)}, u32[]{:S(2)}) %collective-permute-start.1) | collective-permute-done | bytes 802848 | tf_op jit(solution)/shard_map/ppermute | solution.py:287
  29.2 9.4 %collective-permute-start.2 = (bf16[1568,256]{1,0:T(8,128)(2,1)S(1)}, bf16[1568,256]{1,0:T(8,128)(2,1)S(1)}, u32[]{:S(2)}, u32[]{:S(2)}) collective-permute-start(bf16[1568,256]{1,0:T(8,128)(2,1)S(1)} %collective-permute-done.1.fara_ref), channel_id=1, source_target_pairs={{2,3},{3,2},{6,7},{7,6}} | collective-permute-start | bytes 2408456 | tf_op jit(solution)/shard_map/ppermute | solution.py:287
  38.6 4.7 %collective-permute-done.9.fara_ref = bf16[1280,256]{1,0:T(8,128)(2,1)S(1)} collective-permute-done((bf16[1280,256]{1,0:T(8,128)(2,1)}, bf16[1280,256]{1,0:T(8,128)(2,1)S(1)}, u32[]{:S(2)}, u32[]{:S(2)}) %collective-permute-start.9) | collective-permute-done | bytes 655392 | tf_op jit(solution)/shard_map/ppermute | solution.py:287
  43.2 0.0 copy-start.2
  43.2 1.3 collective-permute-start.5
  44.5 12.8 %collective-permute-done.7.fara_ref = bf16[1280,256]{1,0:T(8,128)(2,1)S(1)} collective-permute-done((bf16[1280,256]{1,0:T(8,128)(2,1)}, bf16[1280,256]{1,0:T(8,128)(2,1)S(1)}, u32[]{:S(2)}, u32[]{:S(2)}) %collective-permute-start.7) | collective-permute-done | bytes 655392 | tf_op jit(solution)/shard_map/ppermute | solution.py:287
  57.3 0.0 copy-start
  57.3 1.3 collective-permute-start.3
  58.6 15.6 %collective-permute-done.11.fara_ref = bf16[1536,256]{1,0:T(8,128)(2,1)S(1)} collective-permute-done((bf16[1536,256]{1,0:T(8,128)(2,1)}, bf16[1536,256]{1,0:T(8,128)(2,1)S(1)}, u32[]{:S(2)}, u32[]{:S(2)}) %collective-permute-start.11) | collective-permute-done | bytes 786464 | tf_op jit(solution)/shard_map/ppermute | solution.py:287
  74.1 0.0 copy-done
  74.1 9.4 %collective-permute-start.12 = (bf16[1536,256]{1,0:T(8,128)(2,1)S(1)}, bf16[1536,256]{1,0:T(8,128)(2,1)S(1)}, u32[]{:S(2)}, u32[]{:S(2)}) collective-permute-start(bf16[1536,256]{1,0:T(8,128)(2,1)S(1)} %collective-permute-done.11.fara_ref), channel_id=1, source_target_pairs={{2,3},{3,2},{6,7},{7,6}} | collective-permute-start | bytes 2359304 | tf_op jit(solution)/shard_map/ppermute | solution.py:287
  83.5 0.0 copy-done.2
  83.5 4.8 %collective-permute-done.5.fara_ref = bf16[1280,256]{1,0:T(8,128)(2,1)} collective-permute-done((bf16[1280,256]{1,0:T(8,128)(2,1)}, bf16[1280,256]{1,0:T(8,128)(2,1)}, u32[]{:S(2)}, u32[]{:S(2)}) %collective-permute-start.5) | collective-permute-done | bytes 655392 | tf_op jit(solution)/shard_map/ppermute | solution.py:287
  88.3 9.4 %collective-permute-start.10 = (bf16[1280,256]{1,0:T(8,128)(2,1)}, bf16[1280,256]{1,0:T(8,128)(2,1)S(1)}, u32[]{:S(2)}, u32[]{:S(2)}) collective-permute-start(bf16[1280,256]{1,0:T(8,128)(2,1)} %copy-done.2), channel_id=1, source_target_pairs={{2,3},{3,2},{6,7},{7,6}} | collective-permute-start | bytes 1966088 | tf_op jit(solution)/shard_map/ppermute | solution.py:287
  97.7 4.7 %collective-permute-done.3.fara_ref = bf16[1280,256]{1,0:T(8,128)(2,1)} collective-permute-done((bf16[1280,256]{1,0:T(8,128)(2,1)}, bf16[1280,256]{1,0:T(8,128)(2,1)}, u32[]{:S(2)}, u32[]{:S(2)}) %collective-permute-start.3) | collective-permute-done | bytes 655392 | tf_op jit(solution)/shard_map/ppermute | solution.py:287
  102.3 5.8 %collective-permute-start.8 = (bf16[1280,256]{1,0:T(8,128)(2,1)}, bf16[1280,256]{1,0:T(8,128)(2,1)S(1)}, u32[]{:S(2)}, u32[]{:S(2)}) collective-permute-start(bf16[1280,256]{1,0:T(8,128)(2,1)} %copy-done), channel_id=1, source_target_pairs={{2,3},{3,2},{6,7},{7,6}} | collective-permute-start | bytes 1966088 | tf_op jit(solution)/shard_map/ppermute | solution.py:287
  108.2 0.0 collective-permute-done.2.farb_ref
  108.2 1.9 %collective-permute-start.6 = (bf16[1280,256]{1,0:T(8,128)(2,1)}, bf16[1280,256]{1,0:T(8,128)(2,1)S(1)}, u32[]{:S(2)}, u32[]{:S(2)}) collective-permute-start(bf16[1280,256]{1,0:T(8,128)(2,1)} %collective-permute-done.5.fara_ref), channel_id=1, source_target_pairs={{2,3},{3,2},{6,7},{7,6}} | collective-permute-start | bytes 1966088 | tf_op jit(solution)/shard_map/ppermute | solution.py:287
  110.1 0.0 collective-permute-done.near_ref
  110.1 2.4 %collective-permute-start.4 = (bf16[1280,256]{1,0:T(8,128)(2,1)}, bf16[1280,256]{1,0:T(8,128)(2,1)S(1)}, u32[]{:S(2)}, u32[]{:S(2)}) collective-permute-start(bf16[1280,256]{1,0:T(8,128)(2,1)} %collective-permute-done.3.fara_ref), channel_id=1, source_target_pairs={{2,3},{3,2},{6,7},{7,6}} | collective-permute-start | bytes 1966088 | tf_op jit(solution)/shard_map/ppermute | solution.py:287
  112.5 0.8 subtract_reduce_fusion
  113.4 0.6 fusion.s_hbm
  114.0 0.1 broadcast_in_dim.23.cut_ref
  114.0 9.7 %shard_map.61 = (bf16[32,10,128,256]{3,2,1,0:T(8,128)(2,1)}, f32[10,32,128]{2,1,0:T(8,128)S(1)}, bf16[10,128,256]{2,1,0:T(8,128)(2,1)S(1)}, bf16[4,128,256]{2,1,0:T(8,128)(2,1)S(1)}) custom-call(s32[32]{0:T(128)} %fusion.s_hbm, s32[32,128]{1,0:T(8,128)S(1)} %broadcast_in_dim.23.cut_ref, bf16[32,10,128,256]{3,2,1,0:T(8,128)(2,1)} %bitcast.3, ...), custom_call_target="tpu_custom_call" | custom-call | flops 4026531840 | bytes 7864320 | tf_op jit(solution)/shard_map/pallas_call | solution.py:258
  123.8 0.0 collective-permute-done.12.farb_ref
  123.8 0.0 copy-start.3
  123.8 8.9 %shard_map.62 = (bf16[32,10,128,256]{3,2,1,0:T(8,128)(2,1)}, f32[10,32,128]{2,1,0:T(8,128)S(1)}, bf16[10,128,256]{2,1,0:T(8,128)(2,1)S(1)}, bf16[4,128,256]{2,1,0:T(8,128)(2,1)S(1)}) custom-call(s32[32]{0:T(128)} %fusion.s_hbm, s32[32,128]{1,0:T(8,128)S(1)} %broadcast_in_dim.23.cut_ref, ...), custom_call_target="tpu_custom_call", output_to_operand_aliasing={{0}: (8, {})} | custom-call | flops 4026531840 | bytes 7864320 | tf_op jit(solution)/shard_map/pallas_call | solution.py:258
  132.7 0.0 collective-permute-done.10.farb_ref
  132.7 0.0 copy-done.3
  132.8 0.0 copy-start.1
  132.8 6.6 %shard_map.63 = (bf16[32,10,128,256]{3,2,1,0:T(8,128)(2,1)}, f32[10,32,128]{2,1,0:T(8,128)S(1)}, bf16[10,128,256]{2,1,0:T(8,128)(2,1)S(1)}, bf16[4,128,256]{2,1,0:T(8,128)(2,1)S(1)}) custom-call(s32[32]{0:T(128)} %fusion.s_hbm, s32[32,128]{1,0:T(8,128)S(1)} %broadcast_in_dim.23.cut_ref, ...), custom_call_target="tpu_custom_call", output_to_operand_aliasing={{0}: (8, {})} | custom-call | flops 3355443200 | bytes 6553600 | tf_op jit(solution)/shard_map/pallas_call | solution.py:258
  139.4 0.0 collective-permute-done.8.farb_ref
  139.4 0.0 copy-done.1
  139.4 7.2 %shard_map.64 = (bf16[32,10,128,256]{3,2,1,0:T(8,128)(2,1)}, f32[10,32,128]{2,1,0:T(8,128)S(1)}, bf16[10,128,256]{2,1,0:T(8,128)(2,1)S(1)}, bf16[4,128,256]{2,1,0:T(8,128)(2,1)S(1)}) custom-call(s32[32]{0:T(128)} %fusion.s_hbm, s32[32,128]{1,0:T(8,128)S(1)} %broadcast_in_dim.23.cut_ref, ...), custom_call_target="tpu_custom_call", output_to_operand_aliasing={{0}: (8, {})} | custom-call | flops 3355443200 | bytes 6553600 | tf_op jit(solution)/shard_map/pallas_call | solution.py:258
  146.7 0.0 collective-permute-done.6.farb_ref
  146.7 8.1 %shard_map.65 = (bf16[32,10,128,256]{3,2,1,0:T(8,128)(2,1)}, f32[10,32,128]{2,1,0:T(8,128)S(1)}, bf16[10,128,256]{2,1,0:T(8,128)(2,1)S(1)}, bf16[4,128,256]{2,1,0:T(8,128)(2,1)S(1)}) custom-call(s32[32]{0:T(128)} %fusion.s_hbm, s32[32,128]{1,0:T(8,128)S(1)} %broadcast_in_dim.23.cut_ref, ...), custom_call_target="tpu_custom_call", output_to_operand_aliasing={{0}: (8, {})} | custom-call | flops 3355443200 | bytes 6553600 | tf_op jit(solution)/shard_map/pallas_call | solution.py:258
  154.8 0.0 collective-permute-done.4.farb_ref
  154.8 8.0 %shard_map.66 = (bf16[32,10,128,256]{3,2,1,0:T(8,128)(2,1)}, f32[10,32,128]{2,1,0:T(8,128)}) custom-call(s32[32]{0:T(128)} %fusion.s_hbm, s32[32,128]{1,0:T(8,128)S(1)} %broadcast_in_dim.23.cut_ref, bf16[32,10,128,256]{3,2,1,0:T(8,128)(2,1)} %bitcast.8, bf16[32,128,256]{2,1,0:T(8,128)(2,1)} %k_ref.15, ...), custom_call_target="tpu_custom_call", output_to_operand_aliasing={{0}: (8, {})} | custom-call | flops 3355443200 | bytes 6553600 | tf_op jit(solution)/shard_map/pallas_call | solution.py:258
Async XLA Ops:
  6.6 103.5 %collective-permute-start = (bf16[8224,256]{1,0:T(8,128)(2,1)}, bf16[8224,256]{1,0:T(8,128)(2,1)}, u32[]{:S(2)}, u32[]{:S(2)}) collective-permute-start(bf16[8224,256]{1,0:T(8,128)(2,1)} %get-tuple-element.30), channel_id=1, source_target_pairs={{0,1},{2,3},{4,5},{6,7}} | collective-permute-start | bytes 12632072 | tf_op jit(solution)/shard_map/ppermute | solution.py:287
  10.7 18.5 %collective-permute-start.1 = (bf16[1568,256]{1,0:T(8,128)(2,1)}, bf16[1568,256]{1,0:T(8,128)(2,1)S(1)}, u32[]{:S(2)}, u32[]{:S(2)}) collective-permute-start(bf16[1568,256]{1,0:T(8,128)(2,1)} %shard_map.60), channel_id=1, source_target_pairs={{0,2},{1,3},{4,6},{5,7}} | collective-permute-start | bytes 2408456 | tf_op jit(solution)/shard_map/ppermute | solution.py:287
  12.0 31.2 %collective-permute-start.9 = (bf16[1280,256]{1,0:T(8,128)(2,1)}, bf16[1280,256]{1,0:T(8,128)(2,1)S(1)}, u32[]{:S(2)}, u32[]{:S(2)}) collective-permute-start(bf16[1280,256]{1,0:T(8,128)(2,1)} %get-tuple-element.34), channel_id=1, source_target_pairs={{0,2},{1,3},{4,6},{5,7}} | collective-permute-start | bytes 1966088 | tf_op jit(solution)/shard_map/ppermute | solution.py:287
  13.3 44.0 %collective-permute-start.7 = (bf16[1280,256]{1,0:T(8,128)(2,1)}, bf16[1280,256]{1,0:T(8,128)(2,1)S(1)}, u32[]{:S(2)}, u32[]{:S(2)}) collective-permute-start(bf16[1280,256]{1,0:T(8,128)(2,1)} %get-tuple-element.33), channel_id=1, source_target_pairs={{0,2},{1,3},{4,6},{5,7}} | collective-permute-start | bytes 1966088 | tf_op jit(solution)/shard_map/ppermute | solution.py:287
  14.6 59.5 %collective-permute-start.11 = (bf16[1536,256]{1,0:T(8,128)(2,1)}, bf16[1536,256]{1,0:T(8,128)(2,1)S(1)}, u32[]{:S(2)}, u32[]{:S(2)}) collective-permute-start(bf16[1536,256]{1,0:T(8,128)(2,1)} %get-tuple-element.35), channel_id=1, source_target_pairs={{0,2},{1,3},{4,6},{5,7}} | collective-permute-start | bytes 2359304 | tf_op jit(solution)/shard_map/ppermute | solution.py:287
  29.2 79.0 %collective-permute-start.2 = (bf16[1568,256]{1,0:T(8,128)(2,1)S(1)}, bf16[1568,256]{1,0:T(8,128)(2,1)S(1)}, u32[]{:S(2)}, u32[]{:S(2)}) collective-permute-start(bf16[1568,256]{1,0:T(8,128)(2,1)S(1)} %collective-permute-done.1.fara_ref), channel_id=1, source_target_pairs={{2,3},{3,2},{6,7},{7,6}} | collective-permute-start | bytes 2408456 | tf_op jit(solution)/shard_map/ppermute | solution.py:287
  43.2 40.3 %copy-start.2 = (bf16[1280,256]{1,0:T(8,128)(2,1)}, bf16[1280,256]{1,0:T(8,128)(2,1)S(1)}, u32[]{:S(2)}) copy-start(bf16[1280,256]{1,0:T(8,128)(2,1)S(1)} %collective-permute-done.9.fara_ref) | copy-start | bytes 1966084
  43.2 45.0 %collective-permute-start.5 = (bf16[1280,256]{1,0:T(8,128)(2,1)}, bf16[1280,256]{1,0:T(8,128)(2,1)}, u32[]{:S(2)}, u32[]{:S(2)}) collective-permute-start(bf16[1280,256]{1,0:T(8,128)(2,1)} %get-tuple-element.32), channel_id=1, source_target_pairs={{0,2},{1,3},{4,6},{5,7}} | collective-permute-start | bytes 1966088 | tf_op jit(solution)/shard_map/ppermute | solution.py:287
  57.3 16.9 %copy-start = (bf16[1280,256]{1,0:T(8,128)(2,1)}, bf16[1280,256]{1,0:T(8,128)(2,1)S(1)}, u32[]{:S(2)}) copy-start(bf16[1280,256]{1,0:T(8,128)(2,1)S(1)} %collective-permute-done.7.fara_ref) | copy-start | bytes 1966084
  57.3 45.0 %collective-permute-start.3 = (bf16[1280,256]{1,0:T(8,128)(2,1)}, bf16[1280,256]{1,0:T(8,128)(2,1)}, u32[]{:S(2)}, u32[]{:S(2)}) collective-permute-start(bf16[1280,256]{1,0:T(8,128)(2,1)} %get-tuple-element.31), channel_id=1, source_target_pairs={{0,2},{1,3},{4,6},{5,7}} | collective-permute-start | bytes 1966088 | tf_op jit(solution)/shard_map/ppermute | solution.py:287
  74.1 49.7 %collective-permute-start.12 = (bf16[1536,256]{1,0:T(8,128)(2,1)S(1)}, bf16[1536,256]{1,0:T(8,128)(2,1)S(1)}, u32[]{:S(2)}, u32[]{:S(2)}) collective-permute-start(bf16[1536,256]{1,0:T(8,128)(2,1)S(1)} %collective-permute-done.11.fara_ref), channel_id=1, source_target_pairs={{2,3},{3,2},{6,7},{7,6}} | collective-permute-start | bytes 2359304 | tf_op jit(solution)/shard_map/ppermute | solution.py:287
  88.3 44.4 %collective-permute-start.10 = (bf16[1280,256]{1,0:T(8,128)(2,1)}, bf16[1280,256]{1,0:T(8,128)(2,1)S(1)}, u32[]{:S(2)}, u32[]{:S(2)}) collective-permute-start(bf16[1280,256]{1,0:T(8,128)(2,1)} %copy-done.2), channel_id=1, source_target_pairs={{2,3},{3,2},{6,7},{7,6}} | collective-permute-start | bytes 1966088 | tf_op jit(solution)/shard_map/ppermute | solution.py:287
  102.3 37.1 %collective-permute-start.8 = (bf16[1280,256]{1,0:T(8,128)(2,1)}, bf16[1280,256]{1,0:T(8,128)(2,1)S(1)}, u32[]{:S(2)}, u32[]{:S(2)}) collective-permute-start(bf16[1280,256]{1,0:T(8,128)(2,1)} %copy-done), channel_id=1, source_target_pairs={{2,3},{3,2},{6,7},{7,6}} | collective-permute-start | bytes 1966088 | tf_op jit(solution)/shard_map/ppermute | solution.py:287
  108.2 38.5 %collective-permute-start.6 = (bf16[1280,256]{1,0:T(8,128)(2,1)}, bf16[1280,256]{1,0:T(8,128)(2,1)S(1)}, u32[]{:S(2)}, u32[]{:S(2)}) collective-permute-start(bf16[1280,256]{1,0:T(8,128)(2,1)} %collective-permute-done.5.fara_ref), channel_id=1, source_target_pairs={{2,3},{3,2},{6,7},{7,6}} | collective-permute-start | bytes 1966088 | tf_op jit(solution)/shard_map/ppermute | solution.py:287
  110.1 44.7 %collective-permute-start.4 = (bf16[1280,256]{1,0:T(8,128)(2,1)}, bf16[1280,256]{1,0:T(8,128)(2,1)S(1)}, u32[]{:S(2)}, u32[]{:S(2)}) collective-permute-start(bf16[1280,256]{1,0:T(8,128)(2,1)} %collective-permute-done.3.fara_ref), channel_id=1, source_target_pairs={{2,3},{3,2},{6,7},{7,6}} | collective-permute-start | bytes 1966088 | tf_op jit(solution)/shard_map/ppermute | solution.py:287
  123.8 8.9 %copy-start.3 = (bf16[1280,256]{1,0:T(8,128)(2,1)S(1)}, bf16[1280,256]{1,0:T(8,128)(2,1)}, u32[]{:S(2)}) copy-start(bf16[1280,256]{1,0:T(8,128)(2,1)} %copy-done.2) | copy-start | bytes 1966084
  132.8 6.6 %copy-start.1 = (bf16[1280,256]{1,0:T(8,128)(2,1)S(1)}, bf16[1280,256]{1,0:T(8,128)(2,1)}, u32[]{:S(2)}) copy-start(bf16[1280,256]{1,0:T(8,128)(2,1)} %copy-done) | copy-start | bytes 1966084
